TPU v7x, 32 devices: a whole 2x2x4 slice. The times are simulated.
32 devices in a mesh: tm: 16 (over z, y, x), rows: 2 (over core).
Axes of the slice: x: 2, y: 2, z: 4, core: 2. Of those that a mesh axis runs over, the one named last changes fastest.
Arguments:
- resid: float32 [2, 16, 16, 512], P(None, 'tm', 'rows'), may hold values from -3 to 3
- basis: float32 [4, 2, 16, 16, 512], P(None, None, 'tm', 'rows'), may hold values from -0.01171875 to 0.01171875
Outputs:
- precond: float32 [2, 16, 16, 512], P(None, 'tm', 'rows')
- image: float32 [2, 16, 16, 512], P(None, 'tm', 'rows')
- gram: float32 [5], replicated
All inputs are finite; a program needn't handle non-finite values.
Results may differ from a plain program's by a relative error of at most 0.0005.
Values sent between devices are 32-bit elements; how exact they have to be, the bound alone decides.
A program may use at most 64 MiB of HBM per device.

v0:
```python
import math
import jax
import jax.numpy as jnp
from jax import lax
from jax.sharding import PartitionSpec as P

SWEEPS = 4
ALPHA = 0.01


def padded_2(shard, sides, width):
    for axis, dim in sides:
        count, length = (lax.axis_size(axis), shard.shape[dim])
        up = [(i, (i + 1) % count) for i in range(count - 1)]
        down = [(j, i) for i, j in up]
        last = lax.slice_in_dim(shard, length - width, length, axis=dim)
        first = lax.slice_in_dim(shard, 0, width, axis=dim)
        before = lax.ppermute(last, axis, up)
        after = lax.ppermute(first, axis, down)
        shard = jnp.concatenate([before, shard, after], axis=dim)
    return shard


def shifted(value, axis, steps):
    count = lax.axis_size(axis)
    first, last = (max(0, -steps), min(count, count - steps))
    return lax.ppermute(value, axis, [(source, source + steps) for source in range(first, last)])


def neighbours(padded):
    middle = padded[:, 1:-1]
    sides = jnp.pad(middle, ((0, 0), (0, 0), (1, 1)))
    return padded[:, 2:] + padded[:, :-2] + sides[:, :, 2:] + sides[:, :, :-2]


def cmul(left, right_re, right_im):
    return jnp.stack(
        [left[0] * right_re - left[1] * right_im, left[0] * right_im + left[1] * right_re]
    )


def phases(first, second, steps):
    turns = first * second % steps
    angle = turns.astype(jnp.float32) * (2.0 * math.pi / steps)
    return (jnp.cos(angle), jnp.sin(angle))


def on_device(resid, basis):
    steps = lax.axis_size("tm")
    coupling = 16.0 / (steps * steps)
    me = lax.axis_index("tm")
    rows_dev = resid.shape[2]
    cols = resid.shape[3]
    cells = rows_dev * cols
    piece = cells // steps
    mine = me.astype(jnp.float32)
    gamma = jnp.power(jnp.float32(ALPHA), mine / steps)
    scaled = resid[:, 0] * gamma
    ordinal = jnp.arange(steps, dtype=jnp.int32)
    cos_table, sin_table = phases(ordinal[:, None], ordinal[None, :], steps)
    blocks = lax.all_to_all(
        scaled.reshape(1, 2, cells), "tm", split_axis=2, concat_axis=0, tiled=True
    )
    flat = blocks.reshape(steps, 2 * piece)
    real_part = jnp.dot(cos_table, flat, precision=lax.Precision.HIGHEST)
    imag_part = -jnp.dot(sin_table, flat, precision=lax.Precision.HIGHEST)
    stacked = jnp.stack([real_part, imag_part], 1).reshape(steps, 2, 2, piece)
    spectrum = lax.all_to_all(stacked, "tm", split_axis=0, concat_axis=3, tiled=True)
    rhat = spectrum[0].reshape(2, 2, rows_dev, cols)
    base = jnp.power(jnp.float32(ALPHA), jnp.float32(1.0) / steps)
    angle = mine * (2.0 * math.pi / steps)
    lam_re = 1.0 - base * jnp.cos(angle)
    lam_im = base * jnp.sin(angle)
    disp_spec = rhat[:, 0]
    right = cmul(disp_spec, lam_re, lam_im) + rhat[:, 1]
    den_re = lam_re * lam_re - lam_im * lam_im + 4.0 * coupling
    den_im = 2.0 * lam_re * lam_im
    magnitude = den_re * den_re + den_im * den_im
    inv_re = den_re / magnitude
    inv_im = -den_im / magnitude
    uhat = cmul(right, inv_re, inv_im)
    for sweep in range(SWEEPS - 1):
        padded = padded_2(uhat, (("rows", 1),), 1)
        uhat = cmul(right + coupling * neighbours(padded), inv_re, inv_im)
    vhat = cmul(uhat, lam_re, lam_im) - disp_spec
    yhat = jnp.stack([uhat, vhat], 1)
    spread = lax.all_to_all(
        yhat.reshape(1, 2, 2, cells), "tm", split_axis=3, concat_axis=0, tiled=True
    )
    real_rows = spread[:, 0].reshape(steps, 2 * piece)
    imag_rows = spread[:, 1].reshape(steps, 2 * piece)
    undo = jnp.power(jnp.float32(ALPHA), -ordinal.astype(jnp.float32) / steps) / steps
    history = jnp.dot(cos_table, real_rows, precision=lax.Precision.HIGHEST) - jnp.dot(
        sin_table, imag_rows, precision=lax.Precision.HIGHEST
    )
    history = (history * undo[:, None]).reshape(steps, 2, piece)
    returned = lax.all_to_all(history, "tm", split_axis=0, concat_axis=2, tiled=True)
    precond = returned[0].reshape(2, rows_dev, cols)
    earlier = shifted(precond, "tm", 1)
    disp_rim = padded_2(precond[0:1], (("rows", 1),), 1)
    laplace = neighbours(disp_rim)[0] - 4.0 * precond[0]
    first = precond[0] - earlier[0] - precond[1]
    second = precond[1] - earlier[1] - coupling * laplace
    image = jnp.stack([first, second])
    inner = jnp.sum(basis[:, :, 0] * image[None], axis=(1, 2, 3))
    count = 2.0 * steps * rows_dev * lax.axis_size("rows") * cols
    squares = jnp.sum(image * image) / count
    local_terms = jnp.concatenate([inner, squares[None]])
    gram = lax.psum(local_terms, ("tm", "rows"))
    return (precond[:, None], image[:, None], gram)


def solution(mesh):
    in_specs = (P(None, "tm", "rows", None), P(None, None, "tm", "rows", None))
    out_specs = (P(None, "tm", "rows", None), P(None, "tm", "rows", None), P())
    return jax.shard_map(
        on_device, mesh=mesh, in_specs=in_specs, out_specs=out_specs, check_vma=False
    )
```

profile of v0, /device:TPU:0, one launch (start us, length us, event | category | flops | bytes accessed | tf_op | source)
XLA Modules:
  0.0 169.4 jit_solution(10434036143663607024)
XLA Ops:
  0.7 0.8 broadcast_multiply_fusion
  1.4 0.6 copy.44
  2.1 0.5 broadcast.139
  2.6 19.4 %reduce.4 = f32[4096,2]{1,0:T(8,128)} reduce(f32[4096,1,2]{2,1,0:T(1,128)S(1)} %bitcast.83, f32[]{:T(128)} %broadcast.139), dimensions={1}, to_apply=%bitcast.65.reduce_sub_computation | reduce | bytes 65540
  22.0 3.0 %reshape.138 = f32[16,1,512]{2,1,0:T(1,128)S(1)} reshape(f32[4096,2]{1,0:T(8,128)} %reduce.4) | data formatting | bytes 65536
  25.0 15.5 %all_to_all.63 = f32[16,1,512]{2,1,0:T(1,128)S(1)} all-to-all(f32[16,1,512]{2,1,0:T(1,128)S(1)} %reshape.138), channel_id=1, replica_groups=mesh['tm'=16,'rows'=2] {'tm'}, dimensions={0} | all-to-all | bytes 65536 | tf_op jit(solution)/shard_map/all_to_all | solution.py:61
  40.5 0.7 reduce.5
  41.3 3.4 %reshape.139 = f32[4096,1,2]{2,1,0:T(1,128)S(1)} reshape(f32[16,512]{1,0:T(8,128)S(1)} %reduce.5) | data formatting | bytes 65536
  44.7 0.6 copy.45
  45.3 0.2 convolution_bitcast_fusion
  45.5 0.2 convolution_negate_fusion
  45.8 0.7 copy.48
  46.5 3.5 %all-to-all-start.1 = ((f32[16,2,2,256]{3,2,1,0:T(2,128)}), f32[16,2,2,256]{3,2,1,0:T(2,128)S(1)}, u32[]{:S(2)}, u32[]{:S(2)}) async-start(f32[16,2,2,256]{3,2,1,0:T(2,128)} %copy.48), calls=%async_computation.1 | async-start | bytes 131072 | tf_op jit(solution)/shard_map/all_to_all | solution.py:68
  50.2 7.2 %all-to-all-done.1 = f32[16,2,2,256]{3,2,1,0:T(2,128)S(1)} async-done(((f32[16,2,2,256]{3,2,1,0:T(2,128)}), f32[16,2,2,256]{3,2,1,0:T(2,128)S(1)}, u32[]{:S(2)}, u32[]{:S(2)}) %all-to-all-start.1) | async-done | bytes 65568 | tf_op jit(solution)/shard_map/all_to_all | solution.py:68
  57.6 1.3 collective-permute-start
  58.9 3.0 %collective-permute-start.1 = (f32[2,1,512]{2,1,0:T(1,128)S(1)}, f32[2,1,512]{2,1,0:T(1,128)S(1)}, u32[]{:S(2)}, u32[]{:S(2)}) collective-permute-start(f32[2,1,512]{2,1,0:T(1,128)S(1)} %get-tuple-element.26), channel_id=1, source_target_pairs={{0,1},{2,3},{4,5},{6,7},{8,9},{10,11},{12,13},{14,15},{16,17},{18,... | collective-permute-start | bytes 12296 | tf_op jit(solution)/shard_map/ppermute | solution.py:18
  61.9 0.0 collective-permute-done
  62.0 0.8 collective-permute-done.1
  62.7 0.1 fusion.5
  62.9 1.3 collective-permute-start.2
  64.2 3.0 %collective-permute-start.3 = (f32[2,1,512]{2,1,0:T(1,128)S(1)}, f32[2,1,512]{2,1,0:T(1,128)S(1)}, u32[]{:S(2)}, u32[]{:S(2)}) collective-permute-start(f32[2,1,512]{2,1,0:T(1,128)S(1)} %get-tuple-element.22), channel_id=1, source_target_pairs={{0,1},{2,3},{4,5},{6,7},{8,9},{10,11},{12,13},{14,15},{16,17},{18,... | collective-permute-start | bytes 12296 | tf_op jit(solution)/shard_map/ppermute | solution.py:18
  67.2 0.0 collective-permute-done.2
  67.2 0.8 collective-permute-done.3
  68.0 0.1 fusion.9
  68.1 1.3 collective-permute-start.4
  69.4 3.2 %collective-permute-start.5 = (f32[2,1,512]{2,1,0:T(1,128)S(1)}, f32[2,1,512]{2,1,0:T(1,128)S(1)}, u32[]{:S(2)}, u32[]{:S(2)}) collective-permute-start(f32[2,1,512]{2,1,0:T(1,128)S(1)} %get-tuple-element.18), channel_id=1, source_target_pairs={{0,1},{2,3},{4,5},{6,7},{8,9},{10,11},{12,13},{14,15},{16,17},{18,... | collective-permute-start | bytes 12296 | tf_op jit(solution)/shard_map/ppermute | solution.py:18
  72.6 0.0 collective-permute-done.4
  72.7 0.6 collective-permute-done.5
  73.3 0.1 fusion.13
  73.5 4.4 %copy.51 = f32[1,2,2,4096]{2,1,0,3:T(2,128)} copy(f32[1,2,2,4096]{3,1,2,0:T(2,128)S(1)} %pad_maximum_fusion.1) | data formatting | bytes 131072 | tf_op jit(solution)/shard_map/stack | solution.py:86
  77.9 8.1 %reshape.140 = f32[16,1,1024]{2,1,0:T(1,128)} reshape(f32[4096,1,2,2]{3,2,1,0:T(2,128)} %bitcast.81) | data formatting | bytes 131072
  86.0 3.5 %all-to-all-start.2 = ((f32[16,1,1024]{2,1,0:T(1,128)}), f32[16,1,1024]{2,1,0:T(1,128)S(1)}, u32[]{:S(2)}, u32[]{:S(2)}) async-start(f32[16,1,1024]{2,1,0:T(1,128)} %reshape.140), calls=%async_computation.2 | async-start | bytes 131072 | tf_op jit(solution)/shard_map/all_to_all | solution.py:87
  89.5 7.5 %all-to-all-done.2 = f32[16,1,1024]{2,1,0:T(1,128)S(1)} async-done(((f32[16,1,1024]{2,1,0:T(1,128)}), f32[16,1,1024]{2,1,0:T(1,128)S(1)}, u32[]{:S(2)}, u32[]{:S(2)}) %all-to-all-start.2) | async-done | bytes 65568 | tf_op jit(solution)/shard_map/all_to_all | solution.py:87
  97.0 0.8 reduce.6
  97.8 7.7 %reshape.141 = f32[4096,1,2,2]{3,2,1,0:T(2,128)} reshape(f32[16,1024]{1,0:T(8,128)S(1)} %reduce.6) | data formatting | bytes 131072
  105.6 0.0 copy-start
  105.6 3.6 %copy.57 = f32[1,2,2,16,256]{4,3,2,1,0:T(8,128)S(1)} copy(f32[1,2,2,16,256]{2,1,4,3,0:T(2,128)} %bitcast.82) | data formatting | bytes 131072 | tf_op jit(solution)/shard_map/all_to_all | solution.py:87
  109.2 0.2 fusion.42
  109.5 0.2 fusion
  109.7 10.0 %all_to_all.64 = f32[16,2,256]{2,1,0:T(2,128)S(1)} all-to-all(f32[16,2,256]{2,1,0:T(2,128)S(1)} %reshape.134), channel_id=1, replica_groups=mesh['tm'=16,'rows'=2] {'tm'}, dimensions={0} | all-to-all | bytes 65536 | tf_op jit(solution)/shard_map/all_to_all | solution.py:97
  119.7 0.1 slice_reduce_fusion
  119.8 2.6 %collective-permute-start.6 = (f32[2,8,512]{2,1,0:T(8,128)S(1)}, f32[2,8,512]{2,1,0:T(8,128)S(1)}, u32[]{:S(2)}, u32[]{:S(2)}) collective-permute-start(f32[2,8,512]{2,1,0:T(8,128)S(1)} %reshape_squeeze.15), channel_id=1, source_target_pairs={{0,2},{2,4},{4,6},{6,8},{8,10},{10,12},{12,14},{14,16},{16,18},{18... | collective-permute-start | bytes 98312 | tf_op jit(solution)/shard_map/ppermute | solution.py:27
  122.4 1.3 collective-permute-start.7
  123.7 3.0 %collective-permute-start.8 = (f32[1,1,512]{2,1,0:T(1,128)S(1)}, f32[1,1,512]{2,1,0:T(1,128)S(1)}, u32[]{:S(2)}, u32[]{:S(2)}) collective-permute-start(f32[1,1,512]{2,1,0:T(1,128)S(1)} %get-tuple-element.30), channel_id=1, source_target_pairs={{0,1},{2,3},{4,5},{6,7},{8,9},{10,11},{12,13},{14,15},{16,17},{18,... | collective-permute-start | bytes 6152 | tf_op jit(solution)/shard_map/ppermute | solution.py:18
  126.8 0.0 collective-permute-done.7
  126.8 0.8 collective-permute-done.8
  127.6 0.0 collective-permute-done.6
  127.6 0.1 fusion.26
  127.7 1.2 pad_maximum_fusion.18
  129.5 0.0 copy-done
  129.6 0.1 fusion.1
  129.7 0.1 pad_maximum_fusion.21
  129.8 0.6 broadcast_in_dim_reshape_squeeze.3
  130.4 39.0 %psum.7 = f32[5]{0:T(128)} all-reduce(f32[5]{0:T(128)S(1)} %pad_maximum_fusion.21), channel_id=1, replica_groups=mesh['tm'=16,'rows'=2] {'tm','rows'}, use_global_device_ids=true, to_apply=%region_2.3 | all-reduce | flops 5 | bytes 40 | tf_op jit(solution)/shard_map/psum | solution.py:109
  (36 shorter events, 0.4 us)
Async XLA Ops:
  46.5 11.0 %all-to-all-start.1 = ((f32[16,2,2,256]{3,2,1,0:T(2,128)}), f32[16,2,2,256]{3,2,1,0:T(2,128)S(1)}, u32[]{:S(2)}, u32[]{:S(2)}) async-start(f32[16,2,2,256]{3,2,1,0:T(2,128)} %copy.48), calls=%async_computation.1 | async-start | bytes 131072 | tf_op jit(solution)/shard_map/all_to_all | solution.py:68
  57.6 4.3 %collective-permute-start = (f32[2,1,512]{2,1,0:T(1,128)S(1)}, f32[2,1,512]{2,1,0:T(1,128)S(1)}, u32[]{:S(2)}, u32[]{:S(2)}) collective-permute-start(f32[2,1,512]{2,1,0:T(1,128)S(1)} %get-tuple-element.25), channel_id=1, source_target_pairs={{1,0},{3,2},{5,4},{7,6},{9,8},{11,10},{13,12},{15,14},{17,16},{19,... | collective-permute-start | bytes 12296 | tf_op jit(solution)/shard_map/ppermute | solution.py:19
  58.9 3.8 %collective-permute-start.1 = (f32[2,1,512]{2,1,0:T(1,128)S(1)}, f32[2,1,512]{2,1,0:T(1,128)S(1)}, u32[]{:S(2)}, u32[]{:S(2)}) collective-permute-start(f32[2,1,512]{2,1,0:T(1,128)S(1)} %get-tuple-element.26), channel_id=1, source_target_pairs={{0,1},{2,3},{4,5},{6,7},{8,9},{10,11},{12,13},{14,15},{16,17},{18,... | collective-permute-start | bytes 12296 | tf_op jit(solution)/shard_map/ppermute | solution.py:18
  62.9 4.3 %collective-permute-start.2 = (f32[2,1,512]{2,1,0:T(1,128)S(1)}, f32[2,1,512]{2,1,0:T(1,128)S(1)}, u32[]{:S(2)}, u32[]{:S(2)}) collective-permute-start(f32[2,1,512]{2,1,0:T(1,128)S(1)} %get-tuple-element.21), channel_id=1, source_target_pairs={{1,0},{3,2},{5,4},{7,6},{9,8},{11,10},{13,12},{15,14},{17,16},{19,... | collective-permute-start | bytes 12296 | tf_op jit(solution)/shard_map/ppermute | solution.py:19
  64.2 3.8 %collective-permute-start.3 = (f32[2,1,512]{2,1,0:T(1,128)S(1)}, f32[2,1,512]{2,1,0:T(1,128)S(1)}, u32[]{:S(2)}, u32[]{:S(2)}) collective-permute-start(f32[2,1,512]{2,1,0:T(1,128)S(1)} %get-tuple-element.22), channel_id=1, source_target_pairs={{0,1},{2,3},{4,5},{6,7},{8,9},{10,11},{12,13},{14,15},{16,17},{18,... | collective-permute-start | bytes 12296 | tf_op jit(solution)/shard_map/ppermute | solution.py:18
  68.1 4.5 %collective-permute-start.4 = (f32[2,1,512]{2,1,0:T(1,128)S(1)}, f32[2,1,512]{2,1,0:T(1,128)S(1)}, u32[]{:S(2)}, u32[]{:S(2)}) collective-permute-start(f32[2,1,512]{2,1,0:T(1,128)S(1)} %get-tuple-element.17), channel_id=1, source_target_pairs={{1,0},{3,2},{5,4},{7,6},{9,8},{11,10},{13,12},{15,14},{17,16},{19,... | collective-permute-start | bytes 12296 | tf_op jit(solution)/shard_map/ppermute | solution.py:19
  69.4 3.8 %collective-permute-start.5 = (f32[2,1,512]{2,1,0:T(1,128)S(1)}, f32[2,1,512]{2,1,0:T(1,128)S(1)}, u32[]{:S(2)}, u32[]{:S(2)}) collective-permute-start(f32[2,1,512]{2,1,0:T(1,128)S(1)} %get-tuple-element.18), channel_id=1, source_target_pairs={{0,1},{2,3},{4,5},{6,7},{8,9},{10,11},{12,13},{14,15},{16,17},{18,... | collective-permute-start | bytes 12296 | tf_op jit(solution)/shard_map/ppermute | solution.py:18
  86.0 11.0 %all-to-all-start.2 = ((f32[16,1,1024]{2,1,0:T(1,128)}), f32[16,1,1024]{2,1,0:T(1,128)S(1)}, u32[]{:S(2)}, u32[]{:S(2)}) async-start(f32[16,1,1024]{2,1,0:T(1,128)} %reshape.140), calls=%async_computation.2 | async-start | bytes 131072 | tf_op jit(solution)/shard_map/all_to_all | solution.py:87
  105.6 24.0 %copy-start = (f32[4,2,1,8,512]{4,3,2,1,0:T(8,128)S(1)}, f32[4,2,1,8,512]{4,3,2,1,0:T(8,128)}, u32[]{:S(2)}) copy-start(f32[4,2,1,8,512]{4,3,2,1,0:T(8,128)} %param.3) | copy-start | bytes 393220
  119.8 7.8 %collective-permute-start.6 = (f32[2,8,512]{2,1,0:T(8,128)S(1)}, f32[2,8,512]{2,1,0:T(8,128)S(1)}, u32[]{:S(2)}, u32[]{:S(2)}) collective-permute-start(f32[2,8,512]{2,1,0:T(8,128)S(1)} %reshape_squeeze.15), channel_id=1, source_target_pairs={{0,2},{2,4},{4,6},{6,8},{8,10},{10,12},{12,14},{14,16},{16,18},{18... | collective-permute-start | bytes 98312 | tf_op jit(solution)/shard_map/ppermute | solution.py:27
  122.4 4.4 %collective-permute-start.7 = (f32[1,1,512]{2,1,0:T(1,128)S(1)}, f32[1,1,512]{2,1,0:T(1,128)S(1)}, u32[]{:S(2)}, u32[]{:S(2)}) collective-permute-start(f32[1,1,512]{2,1,0:T(1,128)S(1)} %get-tuple-element.29), channel_id=1, source_target_pairs={{1,0},{3,2},{5,4},{7,6},{9,8},{11,10},{13,12},{15,14},{17,16},{19,... | collective-permute-start | bytes 6152 | tf_op jit(solution)/shard_map/ppermute | solution.py:19
  123.7 3.8 %collective-permute-start.8 = (f32[1,1,512]{2,1,0:T(1,128)S(1)}, f32[1,1,512]{2,1,0:T(1,128)S(1)}, u32[]{:S(2)}, u32[]{:S(2)}) collective-permute-start(f32[1,1,512]{2,1,0:T(1,128)S(1)} %get-tuple-element.30), channel_id=1, source_target_pairs={{0,1},{2,3},{4,5},{6,7},{8,9},{10,11},{12,13},{14,15},{16,17},{18,... | collective-permute-start | bytes 6152 | tf_op jit(solution)/shard_map/ppermute | solution.py:18
where the time goes:
time: 170 us; the launch traced here: 169 us
  blocking collectives  64.5 us (38%)
  local copies, waits for them, and re-layouts  33.7 us (20%)
  starting transfers between devices  27 us (16%)
  other arithmetic  23.6 us (14%)
  waiting for transfers between devices  17.7 us (10%)
  between operations  2.06 us (1%)
    psum x1, blocking collectives, on_device(): gram = lax.psum(local_terms, ('tm', 'rows'))  39 us
    unnamed x10, local copies, waits for them, and re-layouts  22.8 us
    unnamed x1, other arithmetic  19.4 us
    all_to_all x1, blocking collectives, on_device(): lax.all_to_all(scaled.reshape(1, 2, cells), 'tm', split_axis=2, concat_ax...  15.5 us
    ppermute x4, starting transfers between devices, padded_2(): before = lax.ppermute(last, axis, up)  12.3 us
    all_to_all x1, blocking collectives, on_device(): lax.all_to_all(history, 'tm', split_axis=0, concat_axis=2, tiled=True)  9.98 us
    all_to_all x1, waiting for transfers between devices, on_device(): lax.all_to_all(yhat.reshape(1, 2, 2, cells), 'tm', split_axis=3, concat_a...  7.49 us
    all_to_all x1, waiting for transfers between devices, on_device(): lax.all_to_all(stacked, 'tm', split_axis=0, concat_axis=3, tiled=True)  7.25 us
  transfers between devices with their start and end apart: 11, of which 6 were waited for; matrix products, arithmetic and copies ran while one was open for 0% of the time, Pallas kernels for 0%

commit v1 on v0

--- a/solution.py
+++ b/solution.py
@@ -84,8 +84,14 @@
         uhat = cmul(right + coupling * neighbours(padded), inv_re, inv_im)
     vhat = cmul(uhat, lam_re, lam_im) - disp_spec
     yhat = jnp.stack([uhat, vhat], 1)
-    spread = lax.all_to_all(
-        yhat.reshape(1, 2, 2, cells), "tm", split_axis=3, concat_axis=0, tiled=True
+    spread = jnp.concatenate(
+        lax.all_to_all(
+            jnp.stack(jnp.split(yhat.reshape(1, 2, 2, cells), lax.axis_size("tm"), axis=3)),
+            "tm",
+            0,
+            0,
+        ),
+        axis=0,
     )
     real_rows = spread[:, 0].reshape(steps, 2 * piece)
     imag_rows = spread[:, 1].reshape(steps, 2 * piece)

time: 170 us -> 155 us (0.912)
  local copies, waits for them, and re-layouts: 33.7 us -> 19.5 us
    unnamed x10 -> x24, local copies, waits for them, and re-layouts: 22.8 us -> 15.9 us
    another operation x3, local copies, waits for them, and re-layouts: 4.46 us -> 0.07 us  [on_device(): yhat = jnp.stack([uhat, vhat], 1)]
    all_to_all x1 -> x0, local copies, waits for them, and re-layouts: 3.58 us -> none  [on_device(): lax.all_to_all(yhat.reshape(1, 2, 2, cells), 'tm', split_axis=3, concat_a...]
where the time goes in v1:
time: 155 us; the launch traced here: 154 us
  blocking collectives  64.6 us (42%)
  starting transfers between devices  26.8 us (17%)
  other arithmetic  22.8 us (15%)
  local copies, waits for them, and re-layouts  19.5 us (13%)
  waiting for transfers between devices  17.9 us (12%)
  between operations  2 us (1%)
    psum x1, blocking collectives, on_device(): gram = lax.psum(local_terms, ('tm', 'rows'))  39 us
    unnamed x1, other arithmetic  19.4 us
    unnamed x24, local copies, waits for them, and re-layouts  15.9 us
    all_to_all x1, blocking collectives, on_device(): lax.all_to_all(scaled.reshape(1, 2, cells), 'tm', split_axis=2, concat_ax...  15.5 us
    ppermute x4, starting transfers between devices, padded_2(): before = lax.ppermute(last, axis, up)  12.1 us
    all_to_all x1, blocking collectives, on_device(): lax.all_to_all(history, 'tm', split_axis=0, concat_axis=2, tiled=True)  9.98 us
    all_to_all x1, waiting for transfers between devices, on_device(): lax.all_to_all(jnp.stack(jnp.split(yhat.reshape(1, 2, 2, cells), lax.axis...  7.49 us
    all_to_all x1, waiting for transfers between devices, on_device(): lax.all_to_all(stacked, 'tm', split_axis=0, concat_axis=3, tiled=True)  7.25 us
  transfers between devices with their start and end apart: 11, of which 6 were waited for; matrix products, arithmetic and copies ran while one was open for 0% of the time, Pallas kernels for 0%

profile of v1, /device:TPU:0, one launch (start us, length us, event | category | flops | bytes accessed | tf_op | source)
XLA Modules:
  0.0 154.4 jit_solution(12353905935334969767)
XLA Ops:
  0.7 0.8 broadcast_multiply_fusion
  1.4 0.6 copy.21
  2.1 0.5 broadcast.141
  2.6 19.4 %reduce.8 = f32[4096,2]{1,0:T(8,128)} reduce(f32[4096,1,2]{2,1,0:T(1,128)S(1)} %bitcast.136, f32[]{:T(128)} %broadcast.141), dimensions={1}, to_apply=%bitcast.122.reduce_sub_computation | reduce | bytes 65540
  22.0 3.0 %reshape.144 = f32[16,1,512]{2,1,0:T(1,128)S(1)} reshape(f32[4096,2]{1,0:T(8,128)} %reduce.8) | data formatting | bytes 65536
  25.0 15.5 %all_to_all.50 = f32[16,1,512]{2,1,0:T(1,128)S(1)} all-to-all(f32[16,1,512]{2,1,0:T(1,128)S(1)} %reshape.144), channel_id=1, replica_groups=mesh['tm'=16,'rows'=2] {'tm'}, dimensions={0} | all-to-all | bytes 65536 | tf_op jit(solution)/shard_map/all_to_all | solution.py:61
  40.6 0.7 reduce.9
  41.3 3.4 %reshape.145 = f32[4096,1,2]{2,1,0:T(1,128)S(1)} reshape(f32[16,512]{1,0:T(8,128)S(1)} %reduce.9) | data formatting | bytes 65536
  44.7 0.6 copy.22
  45.3 0.2 convolution_bitcast_fusion
  45.5 0.2 convolution_negate_fusion
  45.8 0.7 copy.25
  46.5 3.5 %all-to-all-start.1 = ((f32[16,2,2,256]{3,2,1,0:T(2,128)}), f32[16,2,2,256]{3,2,1,0:T(2,128)S(1)}, u32[]{:S(2)}, u32[]{:S(2)}) async-start(f32[16,2,2,256]{3,2,1,0:T(2,128)} %copy.25), calls=%async_computation.1 | async-start | bytes 131072 | tf_op jit(solution)/shard_map/all_to_all | solution.py:68
  50.2 7.2 %all-to-all-done.1 = f32[16,2,2,256]{3,2,1,0:T(2,128)S(1)} async-done(((f32[16,2,2,256]{3,2,1,0:T(2,128)}), f32[16,2,2,256]{3,2,1,0:T(2,128)S(1)}, u32[]{:S(2)}, u32[]{:S(2)}) %all-to-all-start.1) | async-done | bytes 65568 | tf_op jit(solution)/shard_map/all_to_all | solution.py:68
  57.6 1.3 collective-permute-start
  58.9 3.0 %collective-permute-start.1 = (f32[2,1,512]{2,1,0:T(1,128)S(1)}, f32[2,1,512]{2,1,0:T(1,128)S(1)}, u32[]{:S(2)}, u32[]{:S(2)}) collective-permute-start(f32[2,1,512]{2,1,0:T(1,128)S(1)} %get-tuple-element.26), channel_id=1, source_target_pairs={{0,1},{2,3},{4,5},{6,7},{8,9},{10,11},{12,13},{14,15},{16,17},{18,... | collective-permute-start | bytes 12296 | tf_op jit(solution)/shard_map/ppermute | solution.py:18
  62.0 0.0 collective-permute-done
  62.0 0.8 collective-permute-done.1
  62.8 0.1 fusion.5
  62.9 1.3 collective-permute-start.2
  64.2 3.0 %collective-permute-start.3 = (f32[2,1,512]{2,1,0:T(1,128)S(1)}, f32[2,1,512]{2,1,0:T(1,128)S(1)}, u32[]{:S(2)}, u32[]{:S(2)}) collective-permute-start(f32[2,1,512]{2,1,0:T(1,128)S(1)} %get-tuple-element.22), channel_id=1, source_target_pairs={{0,1},{2,3},{4,5},{6,7},{8,9},{10,11},{12,13},{14,15},{16,17},{18,... | collective-permute-start | bytes 12296 | tf_op jit(solution)/shard_map/ppermute | solution.py:18
  67.2 0.0 collective-permute-done.2
  67.2 0.8 collective-permute-done.3
  68.0 0.1 fusion.9
  68.1 1.3 collective-permute-start.4
  69.4 3.0 %collective-permute-start.5 = (f32[2,1,512]{2,1,0:T(1,128)S(1)}, f32[2,1,512]{2,1,0:T(1,128)S(1)}, u32[]{:S(2)}, u32[]{:S(2)}) collective-permute-start(f32[2,1,512]{2,1,0:T(1,128)S(1)} %get-tuple-element.18), channel_id=1, source_target_pairs={{0,1},{2,3},{4,5},{6,7},{8,9},{10,11},{12,13},{14,15},{16,17},{18,... | collective-permute-start | bytes 12296 | tf_op jit(solution)/shard_map/ppermute | solution.py:18
  72.5 0.0 collective-permute-done.4
  72.5 0.8 collective-permute-done.5
  73.3 0.1 fusion.13
  73.5 0.6 constant_dynamic-update-slice_fusion.17
  74.1 0.6 constant_dynamic-update-slice_fusion.16
  74.7 0.6 constant_dynamic-update-slice_fusion.15
  75.3 0.6 constant_dynamic-update-slice_fusion.14
  75.9 0.6 constant_dynamic-update-slice_fusion.13
  76.5 0.6 constant_dynamic-update-slice_fusion.12
  77.1 0.6 constant_dynamic-update-slice_fusion.11
  77.7 0.6 constant_dynamic-update-slice_fusion.10
  78.2 0.6 constant_dynamic-update-slice_fusion.9
  78.8 0.6 constant_dynamic-update-slice_fusion.8
  79.4 0.6 constant_dynamic-update-slice_fusion.7
  80.0 0.6 constant_dynamic-update-slice_fusion.6
  80.6 0.6 constant_dynamic-update-slice_fusion.5
  81.2 0.6 constant_dynamic-update-slice_fusion.4
  81.8 0.6 constant_dynamic-update-slice_fusion.3
  82.4 0.6 constant_dynamic-update-slice_fusion.2
  83.0 3.5 %all-to-all-start.2 = ((f32[16,1,2,2,256]{4,2,3,1,0:T(2,128)}), f32[16,1,2,2,256]{4,2,3,1,0:T(2,128)S(1)}, u32[]{:S(2)}, u32[]{:S(2)}) async-start(f32[16,1,2,2,256]{4,2,3,1,0:T(2,128)} %constant_dynamic-update-slice_fusion.2), calls=%async_computation.2 | async-start | bytes 131072 | tf_op jit(solution)/shard_map/all_to_all | solution.py:88
  86.5 7.5 %all-to-all-done.2 = f32[16,1,2,2,256]{4,2,3,1,0:T(2,128)S(1)} async-done(((f32[16,1,2,2,256]{4,2,3,1,0:T(2,128)}), f32[16,1,2,2,256]{4,2,3,1,0:T(2,128)S(1)}, u32[]{:S(2)}, u32[]{:S(2)}) %all-to-all-start.2) | async-done | bytes 65568 | tf_op jit(solution)/shard_map/all_to_all | solution.py:88
  94.0 0.2 slice_reduce_fusion
  94.2 0.2 fusion.42
  94.4 0.2 fusion
  94.7 10.0 %all_to_all.51 = f32[16,2,256]{2,1,0:T(2,128)S(1)} all-to-all(f32[16,2,256]{2,1,0:T(2,128)S(1)} %reshape.138), channel_id=1, replica_groups=mesh['tm'=16,'rows'=2] {'tm'}, dimensions={0} | all-to-all | bytes 65536 | tf_op jit(solution)/shard_map/all_to_all | solution.py:103
  104.6 0.1 slice_reduce_fusion.2
  104.8 2.6 %collective-permute-start.6 = (f32[2,8,512]{2,1,0:T(8,128)S(1)}, f32[2,8,512]{2,1,0:T(8,128)S(1)}, u32[]{:S(2)}, u32[]{:S(2)}) collective-permute-start(f32[2,8,512]{2,1,0:T(8,128)S(1)} %reshape_squeeze.15), channel_id=1, source_target_pairs={{0,2},{2,4},{4,6},{6,8},{8,10},{10,12},{12,14},{14,16},{16,18},{18... | collective-permute-start | bytes 98312 | tf_op jit(solution)/shard_map/ppermute | solution.py:27
  107.4 1.3 collective-permute-start.7
  108.7 3.0 %collective-permute-start.8 = (f32[1,1,512]{2,1,0:T(1,128)S(1)}, f32[1,1,512]{2,1,0:T(1,128)S(1)}, u32[]{:S(2)}, u32[]{:S(2)}) collective-permute-start(f32[1,1,512]{2,1,0:T(1,128)S(1)} %get-tuple-element.30), channel_id=1, source_target_pairs={{0,1},{2,3},{4,5},{6,7},{8,9},{10,11},{12,13},{14,15},{16,17},{18,... | collective-permute-start | bytes 6152 | tf_op jit(solution)/shard_map/ppermute | solution.py:18
  111.7 0.0 collective-permute-done.7
  111.7 0.8 collective-permute-done.8
  112.5 0.0 collective-permute-done.6
  112.5 0.1 fusion.26
  112.6 1.2 pad_maximum_fusion.17
  114.5 0.1 fusion.1
  114.6 0.1 pad_maximum_fusion.20
  114.7 0.6 broadcast_in_dim_reshape_squeeze.3
  115.3 39.0 %psum.7 = f32[5]{0:T(128)} all-reduce(f32[5]{0:T(128)S(1)} %pad_maximum_fusion.20), channel_id=1, replica_groups=mesh['tm'=16,'rows'=2] {'tm','rows'}, use_global_device_ids=true, to_apply=%region_2.3 | all-reduce | flops 5 | bytes 40 | tf_op jit(solution)/shard_map/psum | solution.py:115
  (36 shorter events, 0.4 us)
Async XLA Ops:
  45.3 69.2 %copy-start = (f32[4,2,1,8,512]{4,3,2,1,0:T(8,128)S(1)}, f32[4,2,1,8,512]{4,3,2,1,0:T(8,128)}, u32[]{:S(2)}) copy-start(f32[4,2,1,8,512]{4,3,2,1,0:T(8,128)} %param.3) | copy-start | bytes 393220
  46.5 11.0 %all-to-all-start.1 = ((f32[16,2,2,256]{3,2,1,0:T(2,128)}), f32[16,2,2,256]{3,2,1,0:T(2,128)S(1)}, u32[]{:S(2)}, u32[]{:S(2)}) async-start(f32[16,2,2,256]{3,2,1,0:T(2,128)} %copy.25), calls=%async_computation.1 | async-start | bytes 131072 | tf_op jit(solution)/shard_map/all_to_all | solution.py:68
  57.6 4.3 %collective-permute-start = (f32[2,1,512]{2,1,0:T(1,128)S(1)}, f32[2,1,512]{2,1,0:T(1,128)S(1)}, u32[]{:S(2)}, u32[]{:S(2)}) collective-permute-start(f32[2,1,512]{2,1,0:T(1,128)S(1)} %get-tuple-element.25), channel_id=1, source_target_pairs={{1,0},{3,2},{5,4},{7,6},{9,8},{11,10},{13,12},{15,14},{17,16},{19,... | collective-permute-start | bytes 12296 | tf_op jit(solution)/shard_map/ppermute | solution.py:19
  58.9 3.8 %collective-permute-start.1 = (f32[2,1,512]{2,1,0:T(1,128)S(1)}, f32[2,1,512]{2,1,0:T(1,128)S(1)}, u32[]{:S(2)}, u32[]{:S(2)}) collective-permute-start(f32[2,1,512]{2,1,0:T(1,128)S(1)} %get-tuple-element.26), channel_id=1, source_target_pairs={{0,1},{2,3},{4,5},{6,7},{8,9},{10,11},{12,13},{14,15},{16,17},{18,... | collective-permute-start | bytes 12296 | tf_op jit(solution)/shard_map/ppermute | solution.py:18
  62.9 4.3 %collective-permute-start.2 = (f32[2,1,512]{2,1,0:T(1,128)S(1)}, f32[2,1,512]{2,1,0:T(1,128)S(1)}, u32[]{:S(2)}, u32[]{:S(2)}) collective-permute-start(f32[2,1,512]{2,1,0:T(1,128)S(1)} %get-tuple-element.21), channel_id=1, source_target_pairs={{1,0},{3,2},{5,4},{7,6},{9,8},{11,10},{13,12},{15,14},{17,16},{19,... | collective-permute-start | bytes 12296 | tf_op jit(solution)/shard_map/ppermute | solution.py:19
  64.2 3.8 %collective-permute-start.3 = (f32[2,1,512]{2,1,0:T(1,128)S(1)}, f32[2,1,512]{2,1,0:T(1,128)S(1)}, u32[]{:S(2)}, u32[]{:S(2)}) collective-permute-start(f32[2,1,512]{2,1,0:T(1,128)S(1)} %get-tuple-element.22), channel_id=1, source_target_pairs={{0,1},{2,3},{4,5},{6,7},{8,9},{10,11},{12,13},{14,15},{16,17},{18,... | collective-permute-start | bytes 12296 | tf_op jit(solution)/shard_map/ppermute | solution.py:18
  68.1 4.3 %collective-permute-start.4 = (f32[2,1,512]{2,1,0:T(1,128)S(1)}, f32[2,1,512]{2,1,0:T(1,128)S(1)}, u32[]{:S(2)}, u32[]{:S(2)}) collective-permute-start(f32[2,1,512]{2,1,0:T(1,128)S(1)} %get-tuple-element.17), channel_id=1, source_target_pairs={{1,0},{3,2},{5,4},{7,6},{9,8},{11,10},{13,12},{15,14},{17,16},{19,... | collective-permute-start | bytes 12296 | tf_op jit(solution)/shard_map/ppermute | solution.py:19
  69.4 3.8 %collective-permute-start.5 = (f32[2,1,512]{2,1,0:T(1,128)S(1)}, f32[2,1,512]{2,1,0:T(1,128)S(1)}, u32[]{:S(2)}, u32[]{:S(2)}) collective-permute-start(f32[2,1,512]{2,1,0:T(1,128)S(1)} %get-tuple-element.18), channel_id=1, source_target_pairs={{0,1},{2,3},{4,5},{6,7},{8,9},{10,11},{12,13},{14,15},{16,17},{18,... | collective-permute-start | bytes 12296 | tf_op jit(solution)/shard_map/ppermute | solution.py:18
  83.0 11.0 %all-to-all-start.2 = ((f32[16,1,2,2,256]{4,2,3,1,0:T(2,128)}), f32[16,1,2,2,256]{4,2,3,1,0:T(2,128)S(1)}, u32[]{:S(2)}, u32[]{:S(2)}) async-start(f32[16,1,2,2,256]{4,2,3,1,0:T(2,128)} %constant_dynamic-update-slice_fusion.2), calls=%async_computation.2 | async-start | bytes 131072 | tf_op jit(solution)/shard_map/all_to_all | solution.py:88
  104.8 7.8 %collective-permute-start.6 = (f32[2,8,512]{2,1,0:T(8,128)S(1)}, f32[2,8,512]{2,1,0:T(8,128)S(1)}, u32[]{:S(2)}, u32[]{:S(2)}) collective-permute-start(f32[2,8,512]{2,1,0:T(8,128)S(1)} %reshape_squeeze.15), channel_id=1, source_target_pairs={{0,2},{2,4},{4,6},{6,8},{8,10},{10,12},{12,14},{14,16},{16,18},{18... | collective-permute-start | bytes 98312 | tf_op jit(solution)/shard_map/ppermute | solution.py:27
  107.4 4.4 %collective-permute-start.7 = (f32[1,1,512]{2,1,0:T(1,128)S(1)}, f32[1,1,512]{2,1,0:T(1,128)S(1)}, u32[]{:S(2)}, u32[]{:S(2)}) collective-permute-start(f32[1,1,512]{2,1,0:T(1,128)S(1)} %get-tuple-element.29), channel_id=1, source_target_pairs={{1,0},{3,2},{5,4},{7,6},{9,8},{11,10},{13,12},{15,14},{17,16},{19,... | collective-permute-start | bytes 6152 | tf_op jit(solution)/shard_map/ppermute | solution.py:19
  108.7 3.8 %collective-permute-start.8 = (f32[1,1,512]{2,1,0:T(1,128)S(1)}, f32[1,1,512]{2,1,0:T(1,128)S(1)}, u32[]{:S(2)}, u32[]{:S(2)}) collective-permute-start(f32[1,1,512]{2,1,0:T(1,128)S(1)} %get-tuple-element.30), channel_id=1, source_target_pairs={{0,1},{2,3},{4,5},{6,7},{8,9},{10,11},{12,13},{14,15},{16,17},{18,... | collective-permute-start | bytes 6152 | tf_op jit(solution)/shard_map/ppermute | solution.py:18
